TPU v7x, 32 devices: a whole 2x2x4 slice. The times are simulated.
32 devices in a mesh: seq: 16 (over z, x, core), head: 2 (over y).
Axes of the slice: x: 2, y: 2, z: 4, core: 2. Of those that a mesh axis runs over, the one named last changes fastest.
Arguments:
- hidden: bfloat16 [4608, 8192], P('seq'), may hold values from -6 to 6
- norm_gain: bfloat16 [8192], replicated, may hold values from 0.099609375 to 1.8984375
- w_query: bfloat16 [8192, 1024], P('seq', 'head'), may hold values from -0.125 to 0.125
- w_key: bfloat16 [8192, 256], P('seq', 'head'), may hold values from -0.125 to 0.125
- w_value: bfloat16 [8192, 256], P('seq', 'head'), may hold values from -0.0625 to 0.0625
- bias_query: bfloat16 [1024], P('head'), may hold values from -3 to 3
- bias_key: bfloat16 [256], P('head'), may hold values from -200 to 200
- bias_value: bfloat16 [256], P('head'), may hold values from -3 to 3
- w_out: bfloat16 [1024, 8192], P('head', 'seq'), may hold values from -0.1875 to 0.1875
Outputs:
- attn_out: bfloat16 [4608, 8192], P(('seq', 'head'))
All inputs are finite; a program needn't handle non-finite values.
Results may differ from a plain program's by a relative error of at most 0.014.
The roundings to bfloat16 on the way count: a program that leaves them out, or rounds other values in their place, can miss the bound.
Values may be sent and summed in bfloat16 or wider, within the bound.
No kernel may reach another device: no remote copies, remote signals or barrier semaphores. Data moves between devices by JAX's collectives and lax.ppermute only.
A program may use at most 192 MiB of HBM per device.

v0:
```python
import jax
import jax.numpy as jnp
from jax import lax
from jax.sharding import PartitionSpec as P

HEAD_DIM = 128
ROPE_BASE = 1000000.0
EPSILON = 1e-06


def rotary(values, positions):
    half_dim = values.shape[-1] // 2
    freq = ROPE_BASE ** (-2.0 * jnp.arange(half_dim, dtype=jnp.float32) / values.shape[-1])
    angles = positions.astype(jnp.float32)[:, None, None] * freq[None, None, :]
    cosine = jnp.cos(angles)
    sine = jnp.sin(angles)
    first = values[..., :half_dim]
    second = values[..., half_dim:]
    return jnp.concatenate(
        [first * cosine - second * sine, second * cosine + first * sine], axis=-1
    )


def local(hidden, norm_gain, w_query, w_key, w_value, bias_query, bias_key, bias_value, w_out):
    row_count = hidden.shape[0]
    head_count = w_query.shape[1] // HEAD_DIM
    first_row = lax.axis_index("seq") * row_count
    last_row = first_row + row_count - 1
    positions = first_row + jnp.arange(row_count, dtype=jnp.int32)
    widened = hidden.astype(jnp.float32)
    inverse = lax.rsqrt(jnp.mean(widened * widened, axis=-1, keepdims=True) + EPSILON)
    normed = (widened * inverse * norm_gain.astype(jnp.float32)).astype(jnp.bfloat16)
    query = jnp.dot(
        normed,
        lax.all_gather(w_query, "seq", axis=0, tiled=True),
        preferred_element_type=jnp.float32,
    )
    keys = jnp.dot(
        normed, lax.all_gather(w_key, "seq", axis=0, tiled=True), preferred_element_type=jnp.float32
    )
    values = jnp.dot(
        normed,
        lax.all_gather(w_value, "seq", axis=0, tiled=True),
        preferred_element_type=jnp.float32,
    )
    query = query + bias_query.astype(jnp.float32)
    keys = keys + bias_key.astype(jnp.float32)
    values = values + bias_value.astype(jnp.float32)
    query = rotary(query.reshape(row_count, head_count, HEAD_DIM), positions).astype(jnp.bfloat16)
    keys = (
        rotary(keys.reshape(row_count, 1, HEAD_DIM), positions)
        .reshape(row_count, HEAD_DIM)
        .astype(jnp.bfloat16)
    )
    values = values.astype(jnp.bfloat16)
    query_heads = query.transpose(1, 0, 2)
    scaling = HEAD_DIM ** (-0.5)
    initial = (
        jnp.full((head_count, row_count), -1e30, jnp.float32),
        jnp.zeros((head_count, row_count), jnp.float32),
        jnp.zeros((head_count, row_count, HEAD_DIM), jnp.float32),
    )
    key_piece = lax.all_gather(keys, "seq", axis=0, tiled=True)
    value_piece = lax.all_gather(values, "seq", axis=0, tiled=True)

    def update(state):
        highest, total, summed = state
        scores = (
            jnp.einsum("hqd,kd->hqk", query_heads, key_piece, preferred_element_type=jnp.float32)
            * scaling
        )
        key_positions = jnp.arange(key_piece.shape[0], dtype=jnp.int32)
        allowed = positions[:, None] >= key_positions[None, :]
        scores = jnp.where(allowed[None], scores, -jnp.inf)
        new_high = jnp.maximum(highest, jnp.max(scores, axis=-1))
        probs = jnp.exp(scores - new_high[..., None])
        total = jnp.sum(probs, axis=-1)
        mixed = jnp.einsum(
            "hqk,kd->hqd",
            probs.astype(jnp.bfloat16),
            value_piece,
            preferred_element_type=jnp.float32,
        )
        return (new_high, total, mixed)

    def unchanged(state):
        return state

    highest, total, summed = lax.cond(jnp.int32(0) <= last_row, update, unchanged, initial)
    attended = (summed / total[..., None]).astype(jnp.bfloat16)
    attended = attended.transpose(1, 0, 2).reshape(row_count, head_count * HEAD_DIM)
    partial_out = jnp.dot(
        attended,
        lax.all_gather(w_out, "seq", axis=1, tiled=True),
        preferred_element_type=jnp.float32,
    )
    result = lax.psum_scatter(
        partial_out.astype(jnp.bfloat16), "head", scatter_dimension=0, tiled=True
    )
    return result


def solution(mesh):
    in_specs = (
        P("seq", None),
        P(),
        P("seq", "head"),
        P("seq", "head"),
        P("seq", "head"),
        P("head"),
        P("head"),
        P("head"),
        P("head", "seq"),
    )
    out_specs = P(("seq", "head"), None)
    return jax.shard_map(local, mesh=mesh, in_specs=in_specs, out_specs=out_specs, check_vma=False)
```

profile of v0, /device:TPU:0, one launch (start us, length us, event | category | flops | bytes accessed | tf_op | source)
XLA Modules:
  0.0 401.3 jit_solution(17232137514900571910)
XLA Ops:
  6.5 0.7 all-gather.10.cloned.1.call-update
  7.3 0.7 all-gather.12.cloned.1.call-update
  8.1 0.7 all-gather.8.cloned.1.call-update
  8.8 0.7 convert_element_type.48
  9.5 0.7 convert_element_type.52
  10.2 3.4 fusion.11
  13.6 40.1 %all-gather.10.cloned.1.call-done = bf16[8192,128]{1,0:T(8,128)(2,1)} async-done(((bf16[512,128]{1,0:T(8,128)(2,1)}), bf16[8192,128]{1,0:T(8,128)(2,1)}) %all-gather.10.cloned.1.call-update) | async-done | bytes 2097168 | tf_op jit(solution)/shard_map/all_gather | solution.py:39
  53.7 4.6 %fusion.14 = f32[288,1,128]{2,0,1:T(8,128)S(1)} fusion(bf16[8192,128]{1,0:T(8,128)(2,1)} %all-gather.10.cloned.1.call-done, f32[128]{0:T(128)S(1)} %convert_element_type.52, bf16[288,8192]{1,0:T(8,128)(2,1)} %param.11, f32[8192]{0:T(1024)S(1)} %convert_element_type.48, f32[288]{0:T(512)S(1)} %add_rsqrt_fusion), kind=kOutput, calls=%fused_computation.24 | convolution fusion | flops 613453824 | bytes 6997632 | tf_op jit(solution)/shard_map/dot_general | solution.py:38
  58.3 0.7 fusion.24
  58.9 0.7 pad_maximum_fusion
  59.7 0.0 all-gather.14.cloned.1.call-start
  59.8 36.3 %all-gather.12.cloned.1.call-done = bf16[8192,128]{1,0:T(8,128)(2,1)} async-done(((bf16[512,128]{1,0:T(8,128)(2,1)}), bf16[8192,128]{1,0:T(8,128)(2,1)}) %all-gather.12.cloned.1.call-update) | async-done | bytes 2097168 | tf_op jit(solution)/shard_map/all_gather | solution.py:43
  96.1 5.1 %fusion.15 = bf16[288,128]{1,0:T(8,128)(2,1)} fusion(bf16[8192,128]{1,0:T(8,128)(2,1)} %all-gather.12.cloned.1.call-done, f32[128]{0:T(128)S(1)} %convert_element_type.54, bf16[288,8192]{1,0:T(8,128)(2,1)} %param.11, f32[8192]{0:T(1024)S(1)} %convert_element_type.48, f32[288]{0:T(512)S(1)} %add_rsqrt_fusion), kind=kOutput, calls=%fused_computation.25 | convolution fusion | flops 613490688 | bytes 6923904 | tf_op jit(solution)/shard_map/dot_general | solution.py:41
  101.3 0.5 all-gather.16.cloned.1.call-update
  101.8 0.2 reduce-scatter.2.cloned.1.call-start
  102.1 0.6 multiply_cosine_fusion.1
  102.7 68.6 %all-gather.8.cloned.1.call-done = bf16[8192,512]{1,0:T(8,128)(2,1)} async-done(((bf16[512,512]{1,0:T(8,128)(2,1)}), bf16[8192,512]{1,0:T(8,128)(2,1)}) %all-gather.8.cloned.1.call-update) | async-done | bytes 8388624 | tf_op jit(solution)/shard_map/all_gather | solution.py:35
  171.3 7.0 %convolution_add_fusion = f32[288,512]{1,0:T(8,128)S(1)} fusion(bf16[8192,512]{1,0:T(8,128)(2,1)} %all-gather.8.cloned.1.call-done, f32[512]{0:T(512)S(1)} %convert_element_type.50, bf16[288,8192]{1,0:T(8,128)(2,1)} %param.11, f32[8192]{0:T(1024)S(1)} %convert_element_type.48, f32[288]{0:T(512)S(1)} %add_rsqrt_fusion), kind=kOutput, calls=%fused_computation.21 | convolution fusion | flops 2425503744 | bytes 13732992 | tf_op jit(solution)/shard_map/dot_general | solution.py:33
  178.3 0.2 reshape.159
  178.6 0.4 fusion.30
  178.9 0.2 subtract_convert_fusion
  179.1 0.2 maximum_bitcast_fusion
  179.3 31.1 %all-gather.18.cloned.1.call-done = bf16[4608,1,128]{2,0,1:T(8,128)(2,1)} async-done(((bf16[288,1,128]{2,0,1:T(8,128)(2,1)}), bf16[4608,1,128]{2,0,1:T(8,128)(2,1)}) %all-gather.18.cloned.1.call-update) | async-done | bytes 1179664 | tf_op jit(solution)/shard_map/all_gather | solution.py:63
  210.3 39.3 %all-gather.14.cloned.1.call-done = bf16[4608,128]{1,0:T(8,128)(2,1)} async-done(((bf16[288,128]{1,0:T(8,128)(2,1)}), bf16[4608,128]{1,0:T(8,128)(2,1)}) %all-gather.14.cloned.1.call-update) | async-done | bytes 1179664 | tf_op jit(solution)/shard_map/all_gather | solution.py:64
  249.7 19.5 %conditional.1 = (f32[4,288]{1,0:T(4,128)S(1)}, f32[4,288,128]{2,1,0:T(8,128)S(1)}) conditional(s32[]{:T(128)} %convert_element_type.46, () %tuple.13, (s32[]{:T(128)}, s32[288]{0:T(512)S(1)}, bf16[4,288,128]{2,1,0:T(8,128)(2,1)S(1)}, bf16[4608,128]{1,0:T(8,128)(2,1)}, bf16[4608,128]{1,0:T(8,128)(2,1)}) %tuple.36), branch_computations={%region_1.0_spmd, %region_2.5_spmd} | conditional | flops 2777627648 | bytes 72284560 | solution.py:89
  249.7 0.8 iota_compare_fusion
  250.5 5.5 %fusion = (f32[4,288]{1,0:T(4,128)S(1)}, f32[4,288,4608]{2,1,0:T(8,128)S(1)}) fusion(pred[288,4608]{1,0:T(8,128)(4,1)S(1)} %iota_compare_fusion, bf16[4,288,128]{2,1,0:T(8,128)(2,1)S(1)} %get-tuple-element.19, bf16[4608,128]{1,0:T(8,128)(2,1)} %get-tuple-element.20), kind=kOutput, calls=%fused_computation.2 | convolution fusion | flops 1374878592 | bytes 24039936 | tf_op jit(solution)/shard_map/cond/branch_1_fun/hqd,kd->hqk/dot_general | solution.py:69
  255.9 6.6 %fusion.3 = f32[4,288,128]{2,1,0:T(8,128)S(1)} fusion(f32[4,288,4608]{2,1,0:T(8,128)S(1)} %get-tuple-element.27, f32[4,288]{1,0:T(4,128)S(1)} %broadcast_maximum_fusion, pred[288,4608]{1,0:T(8,128)(4,1)S(1)} %iota_compare_fusion, bf16[4608,128]{1,0:T(8,128)(2,1)} %get-tuple-element.21), kind=kOutput, calls=%fused_computation.5 | convolution fusion | flops 1380188160 | bytes 24334848 | tf_op jit(solution)/shard_map/cond/branch_1_fun/hqk,kd->hqd/dot_general | solution.py:78
  262.6 6.6 %fusion.2 = f32[4,288]{1,0:T(4,128)S(1)} fusion(f32[4,288,4608]{2,1,0:T(8,128)S(1)} %get-tuple-element.27, f32[4,288]{1,0:T(4,128)S(1)} %broadcast_maximum_fusion, pred[288,4608]{1,0:T(8,128)(4,1)S(1)} %iota_compare_fusion), kind=kLoop, calls=%fused_computation.4 | loop fusion | flops 21232512 | bytes 22569984 | tf_op jit(solution)/shard_map/cond/branch_1_fun/reduce_sum | solution.py:77
  269.2 59.2 %all-gather.16.cloned.1.call-done = bf16[512,8192]{1,0:T(8,128)(2,1)} async-done(((bf16[512,512]{1,0:T(8,128)(2,1)}), bf16[512,8192]{1,0:T(8,128)(2,1)}) %all-gather.16.cloned.1.call-update) | async-done | bytes 8388624 | tf_op jit(solution)/shard_map/all_gather | solution.py:94
  328.3 7.7 %convolution_convert_fusion = bf16[288,8192]{1,0:T(8,128)(2,1)} fusion(bf16[512,8192]{1,0:T(8,128)(2,1)} %all-gather.16.cloned.1.call-done, f32[4,288,128]{2,1,0:T(8,128)S(1)} %get-tuple-element.24, f32[4,288]{1,0:T(4,128)S(1)} %get-tuple-element.25), kind=kOutput, calls=%fused_computation.17 | convolution fusion | flops 2418573312 | bytes 13701632 | tf_op jit(solution)/shard_map/dot_general | solution.py:92
  336.1 58.4 %reduce-scatter.2.cloned.1.call-done = bf16[144,8192]{1,0:T(8,128)(2,1)} async-done(((bf16[288,8192]{1,0:T(8,128)(2,1)}), bf16[144,8192]{1,0:T(8,128)(2,1)}) %reduce-scatter.2.cloned.1.call-update) | async-done | bytes 2359312 | tf_op jit(solution)/shard_map/reduce_scatter | solution.py:97
  (20 shorter events, 0.3 us)
Async XLA Ops:
  6.5 47.2 %all-gather.10.cloned.1.call-start = ((), (), s32[]{:S(2)}) async-start(), calls=%async_computation.2 | async-start | bytes 2228224 | tf_op jit(solution)/shard_map/all_gather | solution.py:39
  7.3 88.8 %all-gather.12.cloned.1.call-start = ((), (), s32[]{:S(2)}) async-start(), calls=%async_computation.3 | async-start | bytes 2228224 | tf_op jit(solution)/shard_map/all_gather | solution.py:43
  8.0 163.3 %all-gather.8.cloned.1.call-start = ((), (), s32[]{:S(2)}) async-start(), calls=%async_computation.1 | async-start | bytes 8912896 | tf_op jit(solution)/shard_map/all_gather | solution.py:35
  8.7 201.6 %all-gather.18.cloned.1.call-start = ((), (), s32[]{:S(2)}) async-start(), calls=%async_computation.7 | async-start | bytes 1253376 | tf_op jit(solution)/shard_map/all_gather | solution.py:63
  13.5 46.2 %copy-start.1 = (bf16[128]{0:T(256)(128)(2,1)S(1)}, bf16[128]{0:T(256)(128)(2,1)}, u32[]{:S(2)}) copy-start(bf16[128]{0:T(256)(128)(2,1)} %param.18) | copy-start | bytes 772
  58.3 43.8 %copy-start = (bf16[512]{0:T(512)(128)(2,1)S(1)}, bf16[512]{0:T(512)(128)(2,1)}, u32[]{:S(2)}) copy-start(bf16[512]{0:T(512)(128)(2,1)} %param.16) | copy-start | bytes 3076
  59.7 190.0 %all-gather.14.cloned.1.call-start = ((), (), s32[]{:S(2)}) async-start(), calls=%async_computation.4 | async-start | bytes 1253376 | tf_op jit(solution)/shard_map/all_gather | solution.py:64
  101.2 227.1 %all-gather.16.cloned.1.call-start = ((), (), s32[]{:S(2)}) async-start(), calls=%async_computation.5 | async-start | bytes 8912896 | tf_op jit(solution)/shard_map/all_gather | solution.py:94
  101.8 292.6 %reduce-scatter.2.cloned.1.call-start = ((), (), s32[]{:S(2)}) async-start(), calls=%async_computation.6 | async-start | bytes 7077888 | tf_op jit(solution)/shard_map/reduce_scatter | solution.py:97
Sparse Core Ops, SparseCore 0:
  9.5 44.1 all-gather.9
  55.9 40.1 all-gather.11
  98.2 73.0 all-gather.7
  173.4 36.8 all-gather.17
  212.5 37.1 all-gather.13
  251.7 76.5 all-gather.15
  336.2 58.2 reduce-scatter.1
where the time goes:
time: 402 us; the launch traced here: 401 us
  waiting for transfers between devices  336 us (84%)
  matrix products  36.6 us (9%)
  other arithmetic  14.4 us (4%)
  between operations  13.6 us (3%)
    all_gather x1, waiting for transfers between devices, local(): lax.all_gather(w_query, 'seq', axis=0, tiled=True)  68.6 us
    all_gather x1, waiting for transfers between devices, local(): lax.all_gather(w_out, 'seq', axis=1, tiled=True)  59.2 us
    reduce_scatter x1, waiting for transfers between devices, local(): lax.psum_scatter(partial_out.astype(jnp.bfloat16), 'head', scatter_dimens...  58.4 us
    all_gather x1, waiting for transfers between devices, local(): lax.all_gather(w_key, 'seq', axis=0, tiled=True)  40.1 us
    all_gather x1, waiting for transfers between devices, local(): value_piece = lax.all_gather(values, 'seq', axis=0, tiled=True)  39.3 us
    all_gather x1, waiting for transfers between devices, local(): lax.all_gather(w_value, 'seq', axis=0, tiled=True)  36.3 us
    all_gather x1, waiting for transfers between devices, local(): key_piece = lax.all_gather(keys, 'seq', axis=0, tiled=True)  31.1 us
  transfers between devices with their start and end apart: 7, of which 7 were waited for; matrix products, arithmetic and copies ran while one was open for 11% of the time, Pallas kernels for 0%

commit v1 on v0

--- a/solution.py
+++ b/solution.py
@@ -6,6 +6,18 @@
 HEAD_DIM = 128
 ROPE_BASE = 1000000.0
 EPSILON = 1e-06
+
+
+def collect(x, axis, dim):
+    ways, here, lap = (lax.axis_size(axis), lax.axis_index(axis), x.shape[dim])
+    line, have = (x, 1)
+    while have < ways:
+        line = jnp.concatenate(
+            [line, lax.ppermute(line, axis, [(d, (d - have) % ways) for d in range(ways)])],
+            axis=dim,
+        )
+        have = 2 * have
+    return jnp.roll(line, here * lap, axis=dim)
 
 
 def rotary(values, positions):
@@ -61,7 +73,7 @@
         jnp.zeros((head_count, row_count, HEAD_DIM), jnp.float32),
     )
     key_piece = lax.all_gather(keys, "seq", axis=0, tiled=True)
-    value_piece = lax.all_gather(values, "seq", axis=0, tiled=True)
+    value_piece = collect(values, "seq", 0)
 
     def update(state):
         highest, total, summed = state

time: 402 us -> 390 us (0.970)
  waiting for transfers between devices: 336 us -> 311 us
  local copies, waits for them, and re-layouts: 0.59 us -> 7.01 us
    ppermute x0 -> x4, waiting for transfers between devices: none -> 85.4 us  [collect(): lax.ppermute(line, axis, [(d, (d - have) % ways) for d in range(ways)])]
    all_gather x1, waiting for transfers between devices: 68.6 us -> 1.76 us  [local(): lax.all_gather(w_query, 'seq', axis=0, tiled=True)]
    all_gather x1 -> x0, waiting for transfers between devices: 39.3 us -> none  [local(): value_piece = lax.all_gather(values, 'seq', axis=0, tiled=True)]
    unnamed x4 -> x12, local copies, waits for them, and re-layouts: 0.01 us -> 5.59 us
  transfers between devices with their start and end apart: 7 -> 10, of which waited for: 7 -> 10; matrix products, arithmetic and copies ran while one was open for 11% -> 13% of each run, Pallas kernels for 0% -> 0%
where the time goes in v1:
time: 390 us; the launch traced here: 389 us
  waiting for transfers between devices  311 us (80%)
  matrix products  38.8 us (10%)
  other arithmetic  15.2 us (4%)
  between operations  13.6 us (3%)
  local copies, waits for them, and re-layouts  7.01 us (2%)
  starting transfers between devices  3.9 us (1%)
    ppermute x4, waiting for transfers between devices, collect(): lax.ppermute(line, axis, [(d, (d - have) % ways) for d in range(ways)])  85.4 us
    reduce_scatter x1, waiting for transfers between devices, local(): lax.psum_scatter(partial_out.astype(jnp.bfloat16), 'head', scatter_dimens...  58.4 us
    all_gather x1, waiting for transfers between devices, local(): lax.all_gather(w_out, 'seq', axis=1, tiled=True)  57.8 us
    all_gather x1, waiting for transfers between devices, local(): lax.all_gather(w_key, 'seq', axis=0, tiled=True)  40.1 us
    all_gather x1, waiting for transfers between devices, local(): lax.all_gather(w_value, 'seq', axis=0, tiled=True)  35.7 us
    all_gather x1, waiting for transfers between devices, local(): key_piece = lax.all_gather(keys, 'seq', axis=0, tiled=True)  29 us
    dot_general x1, matrix products, local(): jnp.dot(attended, lax.all_gather(w_out, 'seq', axis=1, tiled=True), prefe...  8.48 us
    dot_general x1, matrix products, update(): jnp.einsum('hqk,kd->hqd', probs.astype(jnp.bfloat16), value_piece, prefer...  8.03 us
  transfers between devices with their start and end apart: 10, of which 10 were waited for; matrix products, arithmetic and copies ran while one was open for 13% of the time, Pallas kernels for 0%

profile of v1, /device:TPU:0, one launch (start us, length us, event | category | flops | bytes accessed | tf_op | source)
XLA Modules:
  0.0 389.3 jit_solution(499829141856792588)
XLA Ops:
  6.5 0.7 all-gather.9.cloned.1.call-update
  7.3 0.7 all-gather.11.cloned.1.call-update
  8.1 0.7 all-gather.7.cloned.1.call-update
  8.8 0.7 convert_element_type.51
  10.2 3.4 fusion.13
  13.6 40.1 %all-gather.9.cloned.1.call-done = bf16[8192,128]{1,0:T(8,128)(2,1)} async-done(((bf16[512,128]{1,0:T(8,128)(2,1)}), bf16[8192,128]{1,0:T(8,128)(2,1)}) %all-gather.9.cloned.1.call-update) | async-done | bytes 2097168 | tf_op jit(solution)/shard_map/all_gather | solution.py:51
  53.7 4.6 %fusion.16 = f32[288,1,128]{2,0,1:T(8,128)S(1)} fusion(bf16[8192,128]{1,0:T(8,128)(2,1)} %all-gather.9.cloned.1.call-done, f32[128]{0:T(128)S(1)} %convert_element_type.55, bf16[288,8192]{1,0:T(8,128)(2,1)} %param.11, f32[8192]{0:T(1024)S(1)} %convert_element_type.51, f32[288]{0:T(512)S(1)} %add_rsqrt_fusion), kind=kOutput, calls=%fused_computation.26 | convolution fusion | flops 613453824 | bytes 6997632 | tf_op jit(solution)/shard_map/dot_general | solution.py:50
  58.9 0.7 pad_maximum_fusion.3
  60.3 35.7 %all-gather.11.cloned.1.call-done = bf16[8192,128]{1,0:T(8,128)(2,1)} async-done(((bf16[512,128]{1,0:T(8,128)(2,1)}), bf16[8192,128]{1,0:T(8,128)(2,1)}) %all-gather.11.cloned.1.call-update) | async-done | bytes 2097168 | tf_op jit(solution)/shard_map/all_gather | solution.py:55
  96.1 5.2 %constant_dynamic-update-slice_fusion.9 = (bf16[9216,128]{1,0:T(8,128)(2,1)}, bf16[288,128]{1,0:T(8,128)(2,1)S(1)}) fusion(f32[128]{0:T(128)S(1)} %convert_element_type.57, bf16[8192,128]{1,0:T(8,128)(2,1)} %all-gather.11.cloned.1.call-done, bf16[288,8192]{1,0:T(8,128)(2,1)} %param.11, f32[8192]{0:T(1024)S(1)} %convert_element_type.51, ...), kind=kOutput, calls=%fused_computation.60 | convolution fusion | flops 613490688 | bytes 6997632 | tf_op jit(solution)/shard_map/dot_general | solution.py:53
  101.2 1.9 collective-permute-start
  103.1 2.0 collective-permute-done
  105.1 1.5 collective-permute-start.1
  106.6 7.9 %collective-permute-done.1 = bf16[576,128]{1,0:T(8,128)(2,1)S(1)} collective-permute-done((bf16[576,128]{1,0:T(8,128)(2,1)S(1)}, bf16[576,128]{1,0:T(8,128)(2,1)S(1)}, u32[]{:S(2)}, u32[]{:S(2)}) %collective-permute-start.1) | collective-permute-done | bytes 147488 | tf_op jit(solution)/shard_map/ppermute | solution.py:16
  114.8 19.5 %collective-permute-done.2 = bf16[1152,128]{1,0:T(8,128)(2,1)S(1)} collective-permute-done((bf16[1152,128]{1,0:T(8,128)(2,1)S(1)}, bf16[1152,128]{1,0:T(8,128)(2,1)S(1)}, u32[]{:S(2)}, u32[]{:S(2)}) %collective-permute-start.2) | collective-permute-done | bytes 294944 | tf_op jit(solution)/shard_map/ppermute | solution.py:16
  136.4 0.7 constant_dynamic-update-slice_fusion.6
  137.1 55.9 %collective-permute-done.3 = bf16[2304,128]{1,0:T(8,128)(2,1)S(1)} collective-permute-done((bf16[2304,128]{1,0:T(8,128)(2,1)S(1)}, bf16[2304,128]{1,0:T(8,128)(2,1)S(1)}, u32[]{:S(2)}, u32[]{:S(2)}) %collective-permute-start.3) | collective-permute-done | bytes 589856 | tf_op jit(solution)/shard_map/ppermute | solution.py:16
  193.0 0.9 constant_dynamic-update-slice_fusion.5
  195.8 0.7 constant_dynamic-update-slice_fusion.1
  196.6 0.9 constant_dynamic-update-slice_fusion
  197.4 1.8 all-gather.7.cloned.1.call-done
  199.2 7.0 %convolution_add_fusion = f32[288,512]{1,0:T(8,128)S(1)} fusion(bf16[8192,512]{1,0:T(8,128)(2,1)} %all-gather.7.cloned.1.call-done, f32[512]{0:T(512)S(1)} %convert_element_type.53, bf16[288,8192]{1,0:T(8,128)(2,1)} %param.11, f32[8192]{0:T(1024)S(1)} %convert_element_type.51, f32[288]{0:T(512)S(1)} %add_rsqrt_fusion), kind=kOutput, calls=%fused_computation.23 | convolution fusion | flops 2425503744 | bytes 13732992 | tf_op jit(solution)/shard_map/dot_general | solution.py:45
  207.0 0.9 maximum_bitcast_fusion
  207.9 29.0 %all-gather.15.cloned.1.call-done = bf16[4608,1,128]{2,0,1:T(8,128)(2,1)} async-done(((bf16[288,1,128]{2,0,1:T(8,128)(2,1)}), bf16[4608,1,128]{2,0,1:T(8,128)(2,1)}) %all-gather.15.cloned.1.call-update) | async-done | bytes 1179664 | tf_op jit(solution)/shard_map/all_gather | solution.py:75
  236.9 20.9 %conditional.1 = (f32[4,288]{1,0:T(4,128)S(1)}, f32[4,288,128]{2,1,0:T(8,128)}) conditional(s32[]{:T(128)} %convert_element_type.49, () %tuple.22, (s32[]{:T(128)}, s32[288]{0:T(512)S(1)}, bf16[4,288,128]{2,1,0:T(8,128)(2,1)}, bf16[4608,128]{1,0:T(8,128)(2,1)}, bf16[9216,128]{1,0:T(8,128)(2,1)}) %tuple.44), branch_computations={%region_1.2_spmd, %region_2.5_spmd} | conditional | flops 2777627648 | bytes 72284672 | solution.py:101
  236.9 0.8 iota_compare_fusion
  237.7 5.5 %fusion = (f32[4,288]{1,0:T(4,128)S(1)}, f32[4,288,4608]{2,1,0:T(8,128)S(1)}) fusion(pred[288,4608]{1,0:T(8,128)(4,1)S(1)} %iota_compare_fusion, bf16[4,288,128]{2,1,0:T(8,128)(2,1)} %get-tuple-element.106, bf16[4608,128]{1,0:T(8,128)(2,1)} %get-tuple-element.107), kind=kOutput, calls=%fused_computation.2 | convolution fusion | flops 1374878592 | bytes 24039936 | tf_op jit(solution)/shard_map/cond/branch_1_fun/hqd,kd->hqk/dot_general | solution.py:81
  243.2 8.0 %fusion.3 = f32[4,288,128]{2,1,0:T(8,128)} fusion(f32[4,288,4608]{2,1,0:T(8,128)S(1)} %get-tuple-element.114, f32[4,288]{1,0:T(4,128)S(1)} %broadcast_maximum_fusion, pred[288,4608]{1,0:T(8,128)(4,1)S(1)} %iota_compare_fusion, bf16[9216,128]{1,0:T(8,128)(2,1)} %get-tuple-element.108, s32[]{:T(128)S(6)} %select_n.26), kind=kOutput, calls=%fused_computation.5 | convolution fusion | flops 1380188160 | bytes 24334852 | tf_op jit(solution)/shard_map/cond/branch_1_fun/hqk,kd->hqd/dot_general | solution.py:90
  251.2 6.6 %fusion.2 = f32[4,288]{1,0:T(4,128)S(1)} fusion(f32[4,288,4608]{2,1,0:T(8,128)S(1)} %get-tuple-element.114, f32[4,288]{1,0:T(4,128)S(1)} %broadcast_maximum_fusion, pred[288,4608]{1,0:T(8,128)(4,1)S(1)} %iota_compare_fusion), kind=kLoop, calls=%fused_computation.4 | loop fusion | flops 21232512 | bytes 22569984 | tf_op jit(solution)/shard_map/cond/branch_1_fun/reduce_sum | solution.py:89
  257.8 57.8 %all-gather.13.cloned.1.call-done = bf16[512,8192]{1,0:T(8,128)(2,1)} async-done(((bf16[512,512]{1,0:T(8,128)(2,1)}), bf16[512,8192]{1,0:T(8,128)(2,1)}) %all-gather.13.cloned.1.call-update) | async-done | bytes 8388624 | tf_op jit(solution)/shard_map/all_gather | solution.py:106
  315.5 8.5 %convolution_convert_fusion = bf16[288,8192]{1,0:T(8,128)(2,1)} fusion(bf16[512,8192]{1,0:T(8,128)(2,1)} %all-gather.13.cloned.1.call-done, f32[4,288,128]{2,1,0:T(8,128)} %get-tuple-element.111, f32[4,288]{1,0:T(4,128)S(1)} %get-tuple-element.112), kind=kOutput, calls=%fused_computation.19 | convolution fusion | flops 2418573312 | bytes 13701632 | tf_op jit(solution)/shard_map/dot_general | solution.py:104
  324.0 58.4 %reduce-scatter.2.cloned.1.call-done = bf16[144,8192]{1,0:T(8,128)(2,1)} async-done(((bf16[288,8192]{1,0:T(8,128)(2,1)}), bf16[144,8192]{1,0:T(8,128)(2,1)}) %reduce-scatter.2.cloned.1.call-update) | async-done | bytes 2359312 | tf_op jit(solution)/shard_map/reduce_scatter | solution.py:109
  (37 shorter events, 7.1 us)
Async XLA Ops:
  6.5 47.2 %all-gather.9.cloned.1.call-start = ((), (), s32[]{:S(2)}) async-start(), calls=%async_computation.2 | async-start | bytes 2228224 | tf_op jit(solution)/shard_map/all_gather | solution.py:51
  7.3 88.8 %all-gather.11.cloned.1.call-start = ((), (), s32[]{:S(2)}) async-start(), calls=%async_computation.3 | async-start | bytes 2228224 | tf_op jit(solution)/shard_map/all_gather | solution.py:55
  8.0 191.2 %all-gather.7.cloned.1.call-start = ((), (), s32[]{:S(2)}) async-start(), calls=%async_computation.1 | async-start | bytes 8912896 | tf_op jit(solution)/shard_map/all_gather | solution.py:47
  8.7 228.2 %all-gather.15.cloned.1.call-start = ((), (), s32[]{:S(2)}) async-start(), calls=%async_computation.6 | async-start | bytes 1253376 | tf_op jit(solution)/shard_map/all_gather | solution.py:75
  13.6 46.8 %copy-start.1 = (bf16[128]{0:T(256)(128)(2,1)S(1)}, bf16[128]{0:T(256)(128)(2,1)}, u32[]{:S(2)}) copy-start(bf16[128]{0:T(256)(128)(2,1)} %param.18) | copy-start | bytes 772
  59.7 255.9 %all-gather.13.cloned.1.call-start = ((), (), s32[]{:S(2)}) async-start(), calls=%async_computation.4 | async-start | bytes 8912896 | tf_op jit(solution)/shard_map/all_gather | solution.py:106
  60.3 322.2 %reduce-scatter.2.cloned.1.call-start = ((), (), s32[]{:S(2)}) async-start(), calls=%async_computation.5 | async-start | bytes 7077888 | tf_op jit(solution)/shard_map/reduce_scatter | solution.py:109
  60.3 54.5 %copy-start = (bf16[512]{0:T(512)(128)(2,1)S(1)}, bf16[512]{0:T(512)(128)(2,1)}, u32[]{:S(2)}) copy-start(bf16[512]{0:T(512)(128)(2,1)} %param.16) | copy-start | bytes 3076
  101.2 3.9 collective-permute-start
  105.1 9.4 %collective-permute-start.1 = (bf16[576,128]{1,0:T(8,128)(2,1)S(1)}, bf16[576,128]{1,0:T(8,128)(2,1)S(1)}, u32[]{:S(2)}, u32[]{:S(2)}) collective-permute-start(bf16[576,128]{1,0:T(8,128)(2,1)S(1)} %pad_maximum_fusion.2), channel_id=1, source_target_pairs={{0,28},{2,30},{4,0},{6,2},{8,4},{10,6},{12,8},{14,10},{16,12},{18,... | collective-permute-start | bytes 442376 | tf_op jit(solution)/shard_map/ppermute | solution.py:16
  114.6 19.8 %collective-permute-start.2 = (bf16[1152,128]{1,0:T(8,128)(2,1)S(1)}, bf16[1152,128]{1,0:T(8,128)(2,1)S(1)}, u32[]{:S(2)}, u32[]{:S(2)}) collective-permute-start(bf16[1152,128]{1,0:T(8,128)(2,1)S(1)} %pad_maximum_fusion.1), channel_id=1, source_target_pairs={{0,24},{2,26},{4,28},{6,30},{8,0},{10,2},{12,4},{14,6},{16,8},{18,... | collective-permute-start | bytes 884744 | tf_op jit(solution)/shard_map/ppermute | solution.py:16
  134.4 58.7 %collective-permute-start.3 = (bf16[2304,128]{1,0:T(8,128)(2,1)S(1)}, bf16[2304,128]{1,0:T(8,128)(2,1)S(1)}, u32[]{:S(2)}, u32[]{:S(2)}) collective-permute-start(bf16[2304,128]{1,0:T(8,128)(2,1)S(1)} %pad_maximum_fusion), channel_id=1, source_target_pairs={{0,16},{2,18},{4,20},{6,22},{8,24},{10,26},{12,28},{14,30},{16,0},... | collective-permute-start | bytes 1769480 | tf_op jit(solution)/shard_map/ppermute | solution.py:16
Sparse Core Ops, SparseCore 0:
  9.5 44.1 all-gather.8
  55.9 40.1 all-gather.10
  98.2 100.9 all-gather.6
  201.3 35.5 all-gather.14
  238.9 76.5 all-gather.12
  324.2 58.2 reduce-scatter.1
